TPU v7x, 32 devices: a whole 2x2x4 slice. The times are simulated.
32 devices in a mesh: gx: 8 (over z, core), gz: 4 (over y, x).
Axes of the slice: x: 2, y: 2, z: 4, core: 2. Of those that a mesh axis runs over, the one named last changes fastest.
Arguments:
- populations: float32 [19, 8, 32, 1024], P(None, None, 'gz', 'gx'), may hold values from 0.001 to 0.6, as said below
- solid: int32 [8, 32, 1024], P(None, 'gz', 'gx'), may hold values from 0 to 1, as said below
- top_inflow: float32 [5, 32, 1024], P(None, 'gz', 'gx'), may hold values from 0.005 to 0.1
Outputs:
- advanced: float32 [19, 8, 32, 1024], P(None, None, 'gz', 'gx')
Inputs may be any that keep to these rules, and one draw needn't show every extreme that they name: Positive populations near equilibrium. Only the two planes nearest the wall hold solid nodes.
All inputs are finite; a program needn't handle non-finite values.
Results may differ from a plain program's by a relative error of at most 0.0003.
Values sent between devices are 32-bit elements; how exact they have to be, the bound alone decides.
A program may use at most 64 MiB of HBM per device.

v0:
```python
from functools import reduce

import jax
import jax.numpy as jnp
import numpy as np
from jax import lax
from jax.sharding import PartitionSpec as P

STEPS = 2


lattice = np.array(
    [
        [0, 0, 0],
        [1, 0, 0],
        [-1, 0, 0],
        [0, 1, 0],
        [0, -1, 0],
        [0, 0, 1],
        [0, 0, -1],
        [1, 1, 0],
        [-1, -1, 0],
        [1, -1, 0],
        [-1, 1, 0],
        [1, 0, 1],
        [-1, 0, -1],
        [1, 0, -1],
        [-1, 0, 1],
        [0, 1, 1],
        [0, -1, -1],
        [0, 1, -1],
        [0, -1, 1],
    ]
)
lattice_weights = [1.0 / 3.0] + [1.0 / 18.0] * 6 + [1.0 / 36.0] * 12
opposite = [0, 2, 1, 4, 3, 6, 5, 8, 7, 10, 9, 12, 11, 14, 13, 16, 15, 18, 17]
incoming = [4, 8, 9, 16, 18]
base_drive = 0.0001
drive_gain = 1.0
target_flow = 0.1


def extended(block, sides, width):
    for axis, dim in sides:
        count = lax.axis_size(axis)
        forward = [(i, i + 1) for i in range(count - 1)]
        forward.append((count - 1, 0))
        backward = [(target, source) for source, target in forward]
        low = lax.ppermute(
            lax.slice_in_dim(block, block.shape[dim] - width, None, axis=dim), axis, forward
        )
        high = lax.ppermute(lax.slice_in_dim(block, 0, width, axis=dim), axis, backward)
        block = jnp.concatenate([low, block, high], axis=dim)
    return block


def invert_rows(matrix):
    order = len(matrix)
    work = [
        list(matrix[row]) + [1.0 if col == row else 0.0 for col in range(order)]
        for row in range(order)
    ]
    for col in range(order):
        pivot = max(range(col, order), key=lambda row: abs(work[row][col]))
        work[col], work[pivot] = (work[pivot], work[col])
        lead = work[col][col]
        work[col] = [value / lead for value in work[col]]
        for row in range(order):
            if row != col:
                factor = work[row][col]
                if factor != 0.0:
                    work[row] = [
                        value - factor * other for value, other in zip(work[row], work[col])
                    ]
    return [line[order:] for line in work]


def collide_matrix():
    moment_rows = []
    for power in [
        (0, 0, 0),
        (1, 0, 0),
        (0, 1, 0),
        (0, 0, 1),
        (1, 1, 0),
        (1, 0, 1),
        (0, 1, 1),
        (2, 0, 0),
        (0, 2, 0),
        (0, 0, 2),
        (1, 2, 0),
        (1, 0, 2),
        (2, 1, 0),
        (0, 1, 2),
        (2, 0, 1),
        (0, 2, 1),
        (2, 2, 0),
        (2, 0, 2),
        (0, 2, 2),
    ]:
        moment_rows.append(
            [
                float(
                    int(lattice[q, 0]) ** power[0]
                    * int(lattice[q, 1]) ** power[1]
                    * int(lattice[q, 2]) ** power[2]
                )
                for q in range(19)
            ]
        )
    rates = [0.0] * 4 + [1.8] * 6 + [1.2] * 6 + [1.1] * 3
    inverse = invert_rows(moment_rows)
    result = [
        [
            sum((inverse[row][mid] * rates[mid] * moment_rows[mid][col] for mid in range(19)))
            for col in range(19)
        ]
        for row in range(19)
    ]
    return np.array(result, dtype=np.float32)


def signed_sum(populations, component):
    plus_terms = [populations[index] for index in range(19) if lattice[index, component] == 1]
    minus_terms = [populations[index] for index in range(19) if lattice[index, component] == -1]
    return reduce(lambda left, right: left + right, plus_terms) - reduce(
        lambda left, right: left + right, minus_terms
    )


def moments(populations):
    density = jnp.sum(populations, axis=0)
    momentum = (signed_sum(populations, 0), signed_sum(populations, 1), signed_sum(populations, 2))
    return (density, momentum)


def project(index, velocity):
    result = jnp.zeros_like(velocity[0])
    for component in range(3):
        factor = int(lattice[index, component])
        if factor == 1:
            result = result + velocity[component]
        elif factor == -1:
            result = result - velocity[component]
    return result


def equilibrium(density, velocity):
    speed_square = velocity[0] * velocity[0] + velocity[1] * velocity[1] + velocity[2] * velocity[2]
    terms = []
    for index in range(19):
        along = project(index, velocity)
        terms.append(
            lattice_weights[index]
            * density
            * (1.0 + 3.0 * along + 4.5 * along * along - 1.5 * speed_square)
        )
    return jnp.stack(terms)


def collide(current, density, momentum, driving):
    velocity = tuple((part_value / density for part_value in momentum))
    base_state = equilibrium(density, velocity)
    pushed = equilibrium(density, (velocity[0] + driving / density, velocity[1], velocity[2]))
    relaxed = jnp.tensordot(
        jnp.asarray(collide_matrix()), current - base_state, axes=1, precision=lax.Precision.HIGHEST
    )
    return current - relaxed + pushed - base_state


def extend(collided):
    return extended(collided, (("gx", 3), ("gz", 2)), 1)


def shift_planes(carried, blocked, step_y):
    if step_y == 1:
        carried = jnp.concatenate([jnp.zeros_like(carried[:1]), carried[:-1]], axis=0)
        blocked = jnp.concatenate([jnp.ones_like(blocked[:1]), blocked[:-1]], axis=0)
    elif step_y == -1:
        carried = jnp.concatenate([carried[1:], jnp.zeros_like(carried[:1])], axis=0)
        blocked = jnp.concatenate([blocked[1:], jnp.zeros_like(blocked[:1])], axis=0)
    return (carried, blocked)


def trim(array, cut):
    if cut == 0:
        return array
    return array[..., cut:-cut, cut:-cut]


def stream_block(padded, solid_padded, top_inflow, before):
    planes = padded.shape[1]
    width_z = padded.shape[2] - 2
    width_x = padded.shape[3] - 2
    collided = trim(padded, 1)
    solid = trim(solid_padded, 1)
    results = []
    for index in range(19):
        step_x = int(lattice[index, 0])
        step_y = int(lattice[index, 1])
        step_z = int(lattice[index, 2])
        carried = padded[
            index, :, 1 - step_z : 1 - step_z + width_z, 1 - step_x : 1 - step_x + width_x
        ]
        blocked = solid_padded[
            :, 1 - step_z : 1 - step_z + width_z, 1 - step_x : 1 - step_x + width_x
        ]
        carried, blocked = shift_planes(carried, blocked, step_y)
        arrived = jnp.where(blocked == 1, collided[opposite[index]], carried)
        if step_y == -1:
            arrived = arrived.at[planes - 1].set(top_inflow[incoming.index(index)])
        results.append(arrived)
    return jnp.where(solid[None] == 1, before, jnp.stack(results))


def total_flow(local_sum, node_total):
    return lax.psum(local_sum, ("gx", "gz")) / node_total


def local(populations, solid, top_inflow):
    node_total = float(
        populations.shape[1]
        * populations.shape[2]
        * populations.shape[3]
        * lax.axis_size("gx")
        * lax.axis_size("gz")
    )
    fluid_nodes = (1 - solid).astype(jnp.float32)
    solid_padded = extended(solid, (("gx", 2), ("gz", 1)), 1)
    current = populations
    for step_index in range(STEPS):
        density, momentum = moments(current)
        local_sum = jnp.sum(momentum[0] * fluid_nodes)
        bulk_flow = total_flow(local_sum, node_total)
        driving = base_drive + drive_gain * (target_flow - bulk_flow)
        collided = collide(current, density, momentum, driving)
        padded = extend(collided)
        current = stream_block(padded, solid_padded, top_inflow, current)
    return current


def solution(mesh):
    return jax.shard_map(
        local,
        mesh=mesh,
        in_specs=(P(None, None, "gz", "gx"), P(None, "gz", "gx"), P(None, "gz", "gx")),
        out_specs=P(None, None, "gz", "gx"),
        check_vma=False,
    )
```

profile of v0, /device:TPU:0, one launch (start us, length us, event | category | flops | bytes accessed | tf_op | source)
XLA Modules:
  0.0 149.5 jit_solution(2305365441169737833)
XLA Ops:
  0.0 1.0 fusion.266
  1.0 4.5 %collective-permute-start.2 = (s32[8,8,1]{2,1,0:T(8,128)S(1)}, s32[8,8,1]{2,1,0:T(8,128)S(1)}, u32[]{:S(2)}, u32[]{:S(2)}) collective-permute-start(s32[8,8,1]{2,1,0:T(8,128)S(1)} %get-tuple-element.284), channel_id=1, source_target_pairs={{4,0},{8,4},{12,8},{16,12},{20,16},{24,20},{28,24},{0,28},{5,1},{9... | collective-permute-start | bytes 776 | tf_op jit(solution)/shard_map/ppermute | solution.py:52
  5.5 1.5 %fusion.243 = (f32[]{:T(128)}, f32[1,8,8,128]{3,2,1,0:T(8,128)S(1)}) fusion(s32[8,8,128]{2,1,0:T(8,128)S(1)} %copy-done.1, f32[19,8,8,128]{3,2,1,0:T(8,128)} %param.25), kind=kLoop, calls=%fused_computation.503 | loop fusion | flops 106495 | bytes 393220 | tf_op jit(solution)/shard_map/reduce_sum | solution.py:233
  7.0 1.1 reduce_sum.40
  8.2 39.1 %psum.14 = f32[]{:T(128)} all-reduce(f32[]{:T(128)} %get-tuple-element.179), channel_id=1, replica_groups=mesh['gx'=8,'gz'=4] {'gx','gz'}, use_global_device_ids=true, to_apply=%region_2.0 | all-reduce | flops 1 | bytes 8 | tf_op jit(solution)/shard_map/psum | solution.py:217
  48.8 0.6 copy-done.14
  49.4 1.1 fusion.2
  50.9 1.2 copy.80
  52.6 3.6 %collective-permute-start.3 = (f32[19,8,8,1]{0,2,3,1:T(8,128)S(1)}, f32[19,8,8,1]{0,2,3,1:T(8,128)S(1)}, u32[]{:S(2)}, u32[]{:S(2)}) collective-permute-start(f32[19,8,8,1]{0,2,3,1:T(8,128)S(1)} %copy.82), channel_id=1, source_target_pairs={{4,0},{8,4},{12,8},{16,12},{20,16},{24,20},{28,24},{0,28},{5,1},{9... | collective-permute-start | bytes 14600 | tf_op jit(solution)/shard_map/ppermute | solution.py:52
  56.4 3.4 %collective-permute-start.6 = (s32[8,1,130]{2,1,0:T(1,128)S(1)}, s32[8,1,130]{2,1,0:T(1,128)S(1)}, u32[]{:S(2)}, u32[]{:S(2)}) collective-permute-start(s32[8,1,130]{2,1,0:T(1,128)S(1)} %get-tuple-element.242), channel_id=1, source_target_pairs={{1,0},{2,1},{3,2},{0,3},{5,4},{6,5},{7,6},{4,7},{9,8},{10,9},{11,1... | collective-permute-start | bytes 12488 | tf_op jit(solution)/shard_map/ppermute | solution.py:52
  59.8 0.7 pad_add_fusion.1
  60.5 0.7 fusion.265
  61.2 3.1 %collective-permute-done.4 = s32[8,1,130]{2,1,0:T(1,128)S(1)} collective-permute-done((s32[8,1,130]{2,1,0:T(1,128)S(1)}, s32[8,1,130]{2,1,0:T(1,128)S(1)}, u32[]{:S(2)}, u32[]{:S(2)}) %collective-permute-start.4) | collective-permute-done | bytes 4192 | tf_op jit(solution)/shard_map/ppermute | solution.py:49
  64.4 0.7 fusion.263
  65.2 0.7 copy.83
  65.9 1.5 copy.81
  67.5 1.0 pad_maximum_fusion.3
  68.6 0.7 constant_dynamic-update-slice_fusion.56
  69.3 2.0 %collective-permute-start.5 = (f32[19,8,1,130]{3,2,1,0:T(1,128)S(1)}, f32[19,8,1,130]{3,2,1,0:T(1,128)S(1)}, u32[]{:S(2)}, u32[]{:S(2)}) collective-permute-start(f32[19,8,1,130]{3,2,1,0:T(1,128)S(1)} %get-tuple-element.198), channel_id=1, source_target_pairs={{0,1},{1,2},{2,3},{3,0},{4,5},{5,6},{6,7},{7,4},{8,9},{9,10},{10,1... | collective-permute-start | bytes 237128 | tf_op jit(solution)/shard_map/ppermute | solution.py:49
  71.3 0.6 constant_dynamic-update-slice_fusion.55
  71.9 2.6 %collective-permute-done.7 = f32[19,8,1,130]{3,2,1,0:T(1,128)S(1)} collective-permute-done((f32[19,8,1,130]{3,2,1,0:T(1,128)S(1)}, f32[19,8,1,130]{3,2,1,0:T(1,128)S(1)}, u32[]{:S(2)}, u32[]{:S(2)}) %collective-permute-start.7) | collective-permute-done | bytes 79072 | tf_op jit(solution)/shard_map/ppermute | solution.py:52
  74.5 1.5 %collective-permute-done.5 = f32[19,8,1,130]{3,2,1,0:T(1,128)S(1)} collective-permute-done((f32[19,8,1,130]{3,2,1,0:T(1,128)S(1)}, f32[19,8,1,130]{3,2,1,0:T(1,128)S(1)}, u32[]{:S(2)}, u32[]{:S(2)}) %collective-permute-start.5) | collective-permute-done | bytes 79072 | tf_op jit(solution)/shard_map/ppermute | solution.py:49
  76.9 0.7 copy-done.13
  77.6 0.7 constant_dynamic-update-slice_fusion.53
  78.3 0.7 constant_dynamic-update-slice_fusion.52
  79.6 0.7 copy-done.5
  80.4 0.6 constant_dynamic-update-slice_fusion.48
  81.4 0.6 copy-done.4
  82.1 0.7 copy-done.3
  82.9 0.6 fusion.241
  83.5 38.8 %psum.15 = f32[]{:T(128)} all-reduce(f32[]{:T(128)} %get-tuple-element.131), channel_id=1, replica_groups=mesh['gx'=8,'gz'=4] {'gx','gz'}, use_global_device_ids=true, to_apply=%region_5.6 | all-reduce | flops 1 | bytes 8 | tf_op jit(solution)/shard_map/psum | solution.py:217
  123.9 0.6 copy-done.15
  124.5 1.1 fusion
  127.2 3.5 %collective-permute-start.9 = (f32[19,8,8,1]{0,2,3,1:T(8,128)S(1)}, f32[19,8,8,1]{0,2,3,1:T(8,128)S(1)}, u32[]{:S(2)}, u32[]{:S(2)}) collective-permute-start(f32[19,8,8,1]{0,2,3,1:T(8,128)S(1)} %copy.90), channel_id=1, source_target_pairs={{4,0},{8,4},{12,8},{16,12},{20,16},{24,20},{28,24},{0,28},{5,1},{9... | collective-permute-start | bytes 14600 | tf_op jit(solution)/shard_map/ppermute | solution.py:52
  130.7 0.6 constant_dynamic-update-slice_fusion.115
  131.3 1.0 collective-permute-done.9
  132.3 0.7 copy.91
  133.0 0.7 copy.89
  133.9 1.0 pad_maximum_fusion
  134.9 3.6 %collective-permute-start.11 = (f32[19,8,1,130]{3,2,1,0:T(1,128)S(1)}, f32[19,8,1,130]{3,2,1,0:T(1,128)S(1)}, u32[]{:S(2)}, u32[]{:S(2)}) collective-permute-start(f32[19,8,1,130]{3,2,1,0:T(1,128)S(1)} %get-tuple-element.193), channel_id=1, source_target_pairs={{1,0},{2,1},{3,2},{0,3},{5,4},{6,5},{7,6},{4,7},{9,8},{10,9},{11,1... | collective-permute-start | bytes 237128 | tf_op jit(solution)/shard_map/ppermute | solution.py:52
  138.6 0.6 copy-done.16
  139.3 0.6 copy-done.19
  139.9 3.0 %collective-permute-done.11 = f32[19,8,1,130]{3,2,1,0:T(1,128)S(1)} collective-permute-done((f32[19,8,1,130]{3,2,1,0:T(1,128)S(1)}, f32[19,8,1,130]{3,2,1,0:T(1,128)S(1)}, u32[]{:S(2)}, u32[]{:S(2)}) %collective-permute-start.11) | collective-permute-done | bytes 79072 | tf_op jit(solution)/shard_map/ppermute | solution.py:52
  142.9 2.8 %collective-permute-done.10 = f32[19,8,1,130]{3,2,1,0:T(1,128)S(1)} collective-permute-done((f32[19,8,1,130]{3,2,1,0:T(1,128)S(1)}, f32[19,8,1,130]{3,2,1,0:T(1,128)S(1)}, u32[]{:S(2)}, u32[]{:S(2)}) %collective-permute-start.10) | collective-permute-done | bytes 79072 | tf_op jit(solution)/shard_map/ppermute | solution.py:49
  146.0 0.7 copy-done.17
  146.7 0.6 copy-done.18
  147.5 0.6 copy-done.20
  148.5 0.9 broadcast_select_fusion
  (154 shorter events, 7.6 us)
Async XLA Ops:
  0.0 5.5 %copy-start.1 = (s32[8,8,128]{2,1,0:T(8,128)S(1)}, s32[8,8,128]{2,1,0:T(8,128)}, u32[]{:S(2)}) copy-start(s32[8,8,128]{2,1,0:T(8,128)} %param.26) | copy-start | bytes 98308
  0.0 47.9 %copy-start = (f32[19,8,8,128]{3,2,1,0:T(8,128)S(1)}, f32[19,8,8,128]{3,2,1,0:T(8,128)}, u32[]{:S(2)}) copy-start(f32[19,8,8,128]{3,2,1,0:T(8,128)} %param.25) | copy-start | bytes 1867780
  1.0 55.3 %collective-permute-start.2 = (s32[8,8,1]{2,1,0:T(8,128)S(1)}, s32[8,8,1]{2,1,0:T(8,128)S(1)}, u32[]{:S(2)}, u32[]{:S(2)}) collective-permute-start(s32[8,8,1]{2,1,0:T(8,128)S(1)} %get-tuple-element.284), channel_id=1, source_target_pairs={{4,0},{8,4},{12,8},{16,12},{20,16},{24,20},{28,24},{0,28},{5,1},{9... | collective-permute-start | bytes 776 | tf_op jit(solution)/shard_map/ppermute | solution.py:52
  5.5 50.7 %collective-permute-start = (s32[8,8,1]{2,1,0:T(8,128)S(1)}, s32[8,8,1]{2,1,0:T(8,128)S(1)}, u32[]{:S(2)}, u32[]{:S(2)}) collective-permute-start(s32[8,8,1]{2,1,0:T(8,128)S(1)} %get-tuple-element.285), channel_id=1, source_target_pairs={{0,4},{4,8},{8,12},{12,16},{16,20},{20,24},{24,28},{28,0},{1,5},{5... | collective-permute-start | bytes 776 | tf_op jit(solution)/shard_map/ppermute | solution.py:49
  48.7 0.7 copy-start.14
  52.1 13.8 %collective-permute-start.1 = (f32[19,8,8,1]{0,2,3,1:T(8,128)}, f32[19,8,8,1]{0,2,3,1:T(8,128)}, u32[]{:S(2)}, u32[]{:S(2)}) collective-permute-start(f32[19,8,8,1]{0,2,3,1:T(8,128)} %copy.80), channel_id=1, source_target_pairs={{0,4},{4,8},{8,12},{12,16},{16,20},{20,24},{24,28},{28,0},{1,5},{5... | collective-permute-start | bytes 14600 | tf_op jit(solution)/shard_map/ppermute | solution.py:49
  52.6 12.6 %collective-permute-start.3 = (f32[19,8,8,1]{0,2,3,1:T(8,128)S(1)}, f32[19,8,8,1]{0,2,3,1:T(8,128)S(1)}, u32[]{:S(2)}, u32[]{:S(2)}) collective-permute-start(f32[19,8,8,1]{0,2,3,1:T(8,128)S(1)} %copy.82), channel_id=1, source_target_pairs={{4,0},{8,4},{12,8},{16,12},{20,16},{24,20},{28,24},{0,28},{5,1},{9... | collective-permute-start | bytes 14600 | tf_op jit(solution)/shard_map/ppermute | solution.py:52
  56.4 4.8 %collective-permute-start.6 = (s32[8,1,130]{2,1,0:T(1,128)S(1)}, s32[8,1,130]{2,1,0:T(1,128)S(1)}, u32[]{:S(2)}, u32[]{:S(2)}) collective-permute-start(s32[8,1,130]{2,1,0:T(1,128)S(1)} %get-tuple-element.242), channel_id=1, source_target_pairs={{1,0},{2,1},{3,2},{0,3},{5,4},{6,5},{7,6},{4,7},{9,8},{10,9},{11,1... | collective-permute-start | bytes 12488 | tf_op jit(solution)/shard_map/ppermute | solution.py:52
  59.7 4.5 %collective-permute-start.4 = (s32[8,1,130]{2,1,0:T(1,128)S(1)}, s32[8,1,130]{2,1,0:T(1,128)S(1)}, u32[]{:S(2)}, u32[]{:S(2)}) collective-permute-start(s32[8,1,130]{2,1,0:T(1,128)S(1)} %get-tuple-element.243), channel_id=1, source_target_pairs={{0,1},{1,2},{2,3},{3,0},{4,5},{5,6},{6,7},{7,4},{8,9},{9,10},{10,1... | collective-permute-start | bytes 12488 | tf_op jit(solution)/shard_map/ppermute | solution.py:49
  68.6 2.7 %copy-start.12 = (s32[7,8,128]{2,1,0:T(8,128)S(1)}, s32[7,8,128]{2,1,0:T(8,128)}, u32[]{:S(2)}) copy-start(s32[7,8,128]{2,1,0:T(8,128)} %get-tuple-element.282) | copy-start | bytes 86020
  69.3 5.2 %collective-permute-start.7 = (f32[19,8,1,130]{3,2,1,0:T(1,128)S(1)}, f32[19,8,1,130]{3,2,1,0:T(1,128)S(1)}, u32[]{:S(2)}, u32[]{:S(2)}) collective-permute-start(f32[19,8,1,130]{3,2,1,0:T(1,128)S(1)} %get-tuple-element.197), channel_id=1, source_target_pairs={{1,0},{2,1},{3,2},{0,3},{5,4},{6,5},{7,6},{4,7},{9,8},{10,9},{11,1... | collective-permute-start | bytes 237128 | tf_op jit(solution)/shard_map/ppermute | solution.py:52
  69.3 6.7 %collective-permute-start.5 = (f32[19,8,1,130]{3,2,1,0:T(1,128)S(1)}, f32[19,8,1,130]{3,2,1,0:T(1,128)S(1)}, u32[]{:S(2)}, u32[]{:S(2)}) collective-permute-start(f32[19,8,1,130]{3,2,1,0:T(1,128)S(1)} %get-tuple-element.198), channel_id=1, source_target_pairs={{0,1},{1,2},{2,3},{3,0},{4,5},{5,6},{6,7},{7,4},{8,9},{9,10},{10,1... | collective-permute-start | bytes 237128 | tf_op jit(solution)/shard_map/ppermute | solution.py:49
  76.1 0.7 copy-start.6
  76.1 0.8 copy-start.7
  76.1 0.8 copy-start.8
  76.1 0.8 copy-start.10
  76.1 0.8 copy-start.11
  76.9 0.7 copy-start.13
  78.3 0.7 copy-start.9
  79.6 0.7 copy-start.5
  81.3 0.7 copy-start.4
  82.0 0.7 copy-start.3
  123.8 0.7 copy-start.15
  127.1 5.9 %collective-permute-start.8 = (f32[19,8,8,1]{0,2,3,1:T(8,128)S(1)}, f32[19,8,8,1]{0,2,3,1:T(8,128)S(1)}, u32[]{:S(2)}, u32[]{:S(2)}) collective-permute-start(f32[19,8,8,1]{0,2,3,1:T(8,128)S(1)} %copy.88), channel_id=1, source_target_pairs={{0,4},{4,8},{8,12},{12,16},{16,20},{20,24},{24,28},{28,0},{1,5},{5... | collective-permute-start | bytes 14600 | tf_op jit(solution)/shard_map/ppermute | solution.py:49
  127.2 5.1 %collective-permute-start.9 = (f32[19,8,8,1]{0,2,3,1:T(8,128)S(1)}, f32[19,8,8,1]{0,2,3,1:T(8,128)S(1)}, u32[]{:S(2)}, u32[]{:S(2)}) collective-permute-start(f32[19,8,8,1]{0,2,3,1:T(8,128)S(1)} %copy.90), channel_id=1, source_target_pairs={{4,0},{8,4},{12,8},{16,12},{20,16},{24,20},{28,24},{0,28},{5,1},{9... | collective-permute-start | bytes 14600 | tf_op jit(solution)/shard_map/ppermute | solution.py:52
  133.8 4.7 %copy-start.2 = (f32[19,8,8,128]{3,2,1,0:T(8,128)S(1)}, f32[19,8,8,128]{3,2,1,0:T(8,128)}, u32[]{:S(2)}) copy-start(f32[19,8,8,128]{3,2,1,0:T(8,128)} %constant_dynamic-update-slice_fusion.115) | copy-start | bytes 1867780
  134.9 8.0 %collective-permute-start.11 = (f32[19,8,1,130]{3,2,1,0:T(1,128)S(1)}, f32[19,8,1,130]{3,2,1,0:T(1,128)S(1)}, u32[]{:S(2)}, u32[]{:S(2)}) collective-permute-start(f32[19,8,1,130]{3,2,1,0:T(1,128)S(1)} %get-tuple-element.193), channel_id=1, source_target_pairs={{1,0},{2,1},{3,2},{0,3},{5,4},{6,5},{7,6},{4,7},{9,8},{10,9},{11,1... | collective-permute-start | bytes 237128 | tf_op jit(solution)/shard_map/ppermute | solution.py:52
  138.5 7.2 %collective-permute-start.10 = (f32[19,8,1,130]{3,2,1,0:T(1,128)S(1)}, f32[19,8,1,130]{3,2,1,0:T(1,128)S(1)}, u32[]{:S(2)}, u32[]{:S(2)}) collective-permute-start(f32[19,8,1,130]{3,2,1,0:T(1,128)S(1)} %get-tuple-element.194), channel_id=1, source_target_pairs={{0,1},{1,2},{2,3},{3,0},{4,5},{5,6},{6,7},{7,4},{8,9},{9,10},{10,1... | collective-permute-start | bytes 237128 | tf_op jit(solution)/shard_map/ppermute | solution.py:49
  138.5 0.7 copy-start.16
  139.2 0.7 copy-start.19
  146.0 0.7 copy-start.17
  146.7 0.7 copy-start.18
  147.4 0.7 copy-start.20
  147.4 0.7 copy-start.21
where the time goes:
time: 151 us; the launch traced here: 149 us
  blocking collectives  77.9 us (52%)
  starting transfers between devices  20.7 us (14%)
  local copies, waits for them, and re-layouts  17.8 us (12%)
  other arithmetic  14.9 us (10%)
  waiting for transfers between devices  14 us (9%)
  matrix products  2.11 us (1%)
  between operations  2.08 us (1%)
    psum x2, blocking collectives, total_flow(): return lax.psum(local_sum, ('gx', 'gz')) / node_total  77.9 us
    ppermute x6, starting transfers between devices, extended(): lax.ppermute(lax.slice_in_dim(block, 0, width, axis=dim), axis, backward)  18.6 us
    unnamed x55, local copies, waits for them, and re-layouts  8.54 us
    ppermute x6, waiting for transfers between devices, extended(): lax.ppermute(lax.slice_in_dim(block, block.shape[dim] - width, None, axis...  7.44 us
    ppermute x6, waiting for transfers between devices, extended(): lax.ppermute(lax.slice_in_dim(block, 0, width, axis=dim), axis, backward)  6.59 us
    unnamed x78, other arithmetic  6.22 us
    concatenate x5, other arithmetic, extended(): block = jnp.concatenate([low, block, high], axis=dim)  3.06 us
  transfers between devices with their start and end apart: 12, of which 6 were waited for; matrix products, arithmetic and copies ran while one was open for 8% of the time, Pallas kernels for 0%

commit v1 on v0

v1 whole, which is shorter than its diff:
```python
import functools

import jax
import jax.numpy as jnp
import numpy as np
from jax import lax
from jax.experimental import pallas as pl
from jax.experimental.pallas import tpu as pltpu
from jax.sharding import PartitionSpec as P

STEPS = 2
MESH = pl.DeviceIdType.MESH

lattice = np.array(
    [
        [0, 0, 0],
        [1, 0, 0],
        [-1, 0, 0],
        [0, 1, 0],
        [0, -1, 0],
        [0, 0, 1],
        [0, 0, -1],
        [1, 1, 0],
        [-1, -1, 0],
        [1, -1, 0],
        [-1, 1, 0],
        [1, 0, 1],
        [-1, 0, -1],
        [1, 0, -1],
        [-1, 0, 1],
        [0, 1, 1],
        [0, -1, -1],
        [0, 1, -1],
        [0, -1, 1],
    ]
)
CX = [int(v) for v in lattice[:, 0]]
CY = [int(v) for v in lattice[:, 1]]
CZ = [int(v) for v in lattice[:, 2]]
Q = len(CX)
weights = [1.0 / 3.0] + [1.0 / 18.0] * 6 + [1.0 / 36.0] * 12
opposite = [0, 2, 1, 4, 3, 6, 5, 8, 7, 10, 9, 12, 11, 14, 13, 16, 15, 18, 17]
incoming = [4, 8, 9, 16, 18]
base_drive = 0.0001
drive_gain = 1.0
target_flow = 0.1
RATE_TWO, RATE_ODD, RATE_FOUR = 1.8, 1.2, 1.1

X_DIRS = [[q for q in range(Q) if CX[q] == 1], [q for q in range(Q) if CX[q] == -1]]
Z_DIRS = [[q for q in range(Q) if CZ[q] == 1], [q for q in range(Q) if CZ[q] == -1]]
FACE = len(X_DIRS[0])
Z_FIELDS = FACE + 4
X_FIELDS = 3 * FACE + 1
COMBOS = [(0, 0), (1, 0), (-1, 0), (0, 1), (0, -1), (1, 1), (1, -1), (-1, 1), (-1, -1)]


def push_parts(q):
    w, cx = weights[q], CX[q]
    return (
        w * (4.5 * cx * cx - 1.5),
        3.0 * w * cx,
        9.0 * w * cx * CY[q],
        9.0 * w * cx * CZ[q],
    )


def push(q, square, drive, drive_y, drive_z):
    a, e, b, g = push_parts(q)
    value = a * square
    if e:
        value = value + e * drive
    if b:
        value = value + b * drive_y
    if g:
        value = value + g * drive_z
    return value


def push_linear(q, fields):
    a, e, b, g = push_parts(q)
    value = (2.0 * a) * fields[1] + e
    if b:
        value = value + b * fields[2]
    if g:
        value = value + g * fields[3]
    return value


def collide_base(f):
    s = {q: f[q] + f[q + 1] for q in range(1, Q, 2)}
    t = {q: f[q] - f[q + 1] for q in range(1, Q, 2)}
    plane_p, plane_q, plane_r = s[7] + s[9], s[11] + s[13], s[15] + s[17]
    axes = s[1] + s[3] + s[5]
    density = f[0] + axes + (plane_p + plane_q + plane_r)
    jx = t[1] + (t[7] + t[9]) + (t[11] + t[13])
    jy = t[3] + (t[7] - t[9]) + (t[15] + t[17])
    jz = t[5] + (t[11] - t[13]) + (t[15] - t[17])
    inverse = 1.0 / density
    ux, uy, uz = jx * inverse, jy * inverse, jz * inverse
    exx, eyy, ezz = jx * ux, jy * uy, jz * uz
    shared = density * (1.0 / 9.0) - (exx + eyy + ezz) * (1.0 / 6.0)
    hx, hy, hz = 0.5 * exx, 0.5 * eyy, 0.5 * ezz
    dp = plane_p - (shared + (hx + hy))
    dq = plane_q - (shared + (hx + hz))
    dr = plane_r - (shared + (hy + hz))
    mix = RATE_TWO - RATE_FOUR
    ax = s[1] - RATE_TWO * (s[1] - (shared + hx)) - mix * (dp + dq)
    ay = s[3] - RATE_TWO * (s[3] - (shared + hy)) - mix * (dp + dr)
    az = s[5] - RATE_TWO * (s[5] - (shared + hz)) - mix * (dq + dr)
    op, oq, orr = plane_p - RATE_FOUR * dp, plane_q - RATE_FOUR * dq, plane_r - RATE_FOUR * dr
    out = [None] * Q
    out[0] = density - ((ax + ay + az) + (op + oq + orr))
    keep = 0.5 * (1.0 - RATE_ODD)
    third, sixth = 0.5 * RATE_ODD / 3.0, 0.5 * RATE_ODD / 6.0
    for q, even, flow in ((1, ax, jx), (3, ay, jy), (5, az, jz)):
        half = 0.5 * even
        odd = keep * t[q] + third * flow
        out[q], out[q + 1] = half + odd, half - odd
    sx, sy, sz = sixth * jx, sixth * jy, sixth * jz
    for q, even, cross, one, two in (
        (7, op, jx * uy, sx, sy),
        (11, oq, jx * uz, sx, sz),
        (15, orr, jy * uz, sy, sz),
    ):
        delta = s[q] - s[q + 2]
        delta = 0.25 * (delta - RATE_TWO * (delta - cross))
        quarter = 0.25 * even
        for index, part, flow in ((q, quarter + delta, one + two), (q + 2, quarter - delta, one - two)):
            odd = keep * t[index] + flow
            out[index], out[index + 1] = part + odd, part - odd
    return out, (inverse, ux, uy, uz)


def kernel(
    sizes,
    pop_hbm,
    solid_hbm,
    inflow_hbm,
    out_ref,
    pop,
    solid_in,
    inflow,
    flags,
    masks,
    base,
    fields,
    done,
    state,
    z_send,
    z_recv,
    x_send,
    x_recv,
    a_send,
    a_recv,
    load_sem,
    z_send_sem,
    z_recv_sem,
    x_send_sem,
    x_recv_sem,
    a_send_sem,
    a_recv_sem,
):
    planes, rows, width, count_x, count_z = sizes
    total_devices = count_x * count_z
    gx, gz = lax.axis_index("gx"), lax.axis_index("gz")
    me = gx * count_z + gz

    def peer(offset):
        rank = lax.rem(me + offset, total_devices)
        return {"gx": lax.div(rank, count_z), "gz": lax.rem(rank, count_z)}

    def beside(step_x, step_z):
        return {
            "gx": lax.rem(gx + (step_x + count_x), count_x),
            "gz": lax.rem(gz + (step_z + count_z), count_z),
        }

    def each_peer(body):
        if total_devices <= 64:
            for j in range(total_devices - 1):
                body(j)
        else:

            def step(j, carry):
                body(j)
                return carry

            lax.fori_loop(0, total_devices - 1, step, 0)

    loads = [
        pltpu.make_async_copy(solid_hbm, solid_in, load_sem.at[0]),
        pltpu.make_async_copy(pop_hbm, pop, load_sem.at[1]),
        pltpu.make_async_copy(inflow_hbm, inflow, load_sem.at[2]),
    ]
    for load in loads:
        load.start()
    barrier = pltpu.get_barrier_semaphore()
    each_peer(
        lambda j: pl.semaphore_signal(barrier, inc=1, device_id=peer(j + 1), device_id_type=MESH)
    )

    lane = lax.broadcasted_iota(jnp.int32, (planes, width), 1)
    height = lax.broadcasted_iota(jnp.int32, (planes, width), 0)

    def turn(tile, shift, axis):
        shift = shift % tile.shape[axis]
        return pltpu.roll(tile, shift, axis) if shift else tile

    def strided(q, z):
        return pl.ds(q * planes * rows + z, planes, stride=rows)

    def current(step, q, z):
        return pop[strided(q, z), :] if step == 0 else state[z, q]

    def send_flow(step, acc):
        a_send[step] = jnp.sum(acc, axis=0, keepdims=True)

    def flow_copy(step, j):
        return pltpu.make_async_remote_copy(
            src_ref=a_send.at[step],
            dst_ref=a_recv.at[step, j],
            send_sem=a_send_sem.at[step],
            recv_sem=a_recv_sem.at[step],
            device_id=peer(j + 1),
            device_id_type=MESH,
        )

    def z_copy(step, side):
        return pltpu.make_async_remote_copy(
            src_ref=z_send.at[step, side],
            dst_ref=z_recv.at[step, side],
            send_sem=z_send_sem.at[step, side],
            recv_sem=z_recv_sem.at[step, side],
            device_id=beside(0, 1 - 2 * side),
            device_id_type=MESH,
        )

    def x_copy(step, side, k):
        slot = 1 - k
        return pltpu.make_async_remote_copy(
            src_ref=x_send.at[step, side],
            dst_ref=x_recv.at[step, side, slot],
            send_sem=x_send_sem.at[step, side, slot],
            recv_sem=x_recv_sem.at[step, side, slot],
            device_id=beside(1 - 2 * side, k),
            device_id_type=MESH,
        )

    x_order = [(side, k) for k in (1, -1, 0) for side in (0, 1)]

    def collide_all(step, after_edges):
        packs = [jnp.zeros((planes, width), jnp.float32) for _ in range(2)]
        order = [rows - 1, 0] + list(range(1, rows - 1))
        for place, z in enumerate(order):
            f = [current(step, q, z) for q in range(Q)]
            out, parts = collide_base(f)
            solid = flags[z + 1]
            for q in range(Q):
                base[z, q] = out[q]
            for i in range(4):
                fields[z, i] = parts[i]
            for side in range(2):
                if z == (rows - 1 if side == 0 else 0):
                    sent = [out[q] for q in Z_DIRS[side]] + [parts[0], parts[1], parts[3], solid]
                    for i, tile in enumerate(sent):
                        z_send[step, side, i] = tile
                edge = width - 1 if side == 0 else 0
                sent = [out[q] for q in X_DIRS[side]]
                sent += [push_linear(q, parts) for q in X_DIRS[side]]
                sent += [push_parts(q)[0] * parts[0] for q in X_DIRS[side]]
                sent += [solid]
                for i, tile in enumerate(sent):
                    to = i * rows + z
                    packs[side] = jnp.where(lane == to, turn(tile, to - edge, 1), packs[side])
            if place == 1:
                after_edges()
        for side in range(2):
            x_send[step, side] = packs[side]

    def x_edge(finished, side, index, row):
        slot = 0 if row < 0 else (2 if row >= rows else 1)
        at = index * rows + row % rows
        to = 0 if side == 0 else width - 1
        return turn(finished[side][slot], to - at, 1), lane == to

    def moved(tile, finished, index, row, cx):
        if cx:
            side = 0 if cx == 1 else 1
            value, where = x_edge(finished, side, index, row)
            tile = jnp.where(where, value, turn(tile, cx, 1))
        return tile

    loads[0].wait()
    for z in range(rows):
        flags[z + 1] = solid_in[pl.ds(z, planes, stride=rows), :].astype(jnp.float32)
    loads[1].wait()
    acc = jnp.zeros((planes, width), jnp.float32)
    for z in range(rows):
        plus = [pop[strided(q, z), :] for q in X_DIRS[0]]
        minus = [pop[strided(q, z), :] for q in X_DIRS[1]]
        jx = functools.reduce(lambda l, r: l + r, [p - m for p, m in zip(plus, minus)])
        acc = acc + jx * (1.0 - flags[z + 1])
    send_flow(0, acc)
    collide_all(0, lambda: None)
    loads[2].wait()
    pl.semaphore_wait(barrier, total_devices - 1)
    each_peer(lambda j: flow_copy(0, j).start())
    for side in range(2):
        z_copy(0, side).start()
    for side, k in x_order:
        x_copy(0, side, k).start()

    for step in range(STEPS):
        for side in range(2):
            z_copy(step, side).wait_recv()
        for side, k in x_order:
            x_copy(step, side, k).wait_recv()
        if step == 0:
            flags[0] = z_recv[0, 0, Z_FIELDS - 1]
            flags[rows + 1] = z_recv[0, 1, Z_FIELDS - 1]
            raw = [[x_recv[0, side, slot] for slot in range(3)] for side in range(2)]
            for row in range(-1, rows + 1):
                tile = flags[row + 1]
                for cx in (0, 1, -1):
                    shifted = moved(tile, raw, X_FIELDS - 1, row, cx)
                    for cy in (0, 1, -1):
                        if (row < 0 or row >= rows) and cx and cy:
                            continue
                        value = turn(shifted, cy, 0)
                        if cy == 1:
                            value = jnp.where(height == 0, 1.0, value)
                        elif cy == -1:
                            value = jnp.where(height == planes - 1, 0.0, value)
                        masks[row + 1, COMBOS.index((cx, cy))] = value

        pltpu.make_async_copy(a_recv.at[step], a_recv.at[step], a_recv_sem.at[step]).wait()
        flow = a_send[step] + jnp.sum(a_recv[step], axis=0)
        flow = jnp.sum(flow, axis=1, keepdims=True)
        bulk = flow / float(planes * rows * width * total_devices)
        drive = jnp.broadcast_to(base_drive + drive_gain * (target_flow - bulk), (planes, width))

        for z in range(rows):
            inverse, ux, uy, uz = (fields[z, i] for i in range(4))
            square = drive * (2.0 * ux + drive * inverse)
            drive_y, drive_z = drive * uy, drive * uz
            for q in range(Q):
                done[z + 1, q] = base[z, q] + push(q, square, drive, drive_y, drive_z)
        for side in range(2):
            row = 0 if side == 0 else rows + 1
            inverse, ux, uz = (z_recv[step, side, FACE + i] for i in range(3))
            square = drive * (2.0 * ux + drive * inverse)
            drive_z = drive * uz
            for i, q in enumerate(Z_DIRS[side]):
                done[row, q] = z_recv[step, side, i] + push(q, square, drive, None, drive_z)
        finished = []
        for side in range(2):
            tiles = []
            for slot in range(3):
                tile = x_recv[step, side, slot]
                linear = turn(tile, -FACE * rows, 1)
                second = turn(tile, -2 * FACE * rows, 1)
                tiles.append(tile + drive * (linear + drive * second))
            finished.append(tiles)

        acc = jnp.zeros((planes, width), jnp.float32)
        for z in range(rows):
            solid = flags[z + 1] > 0.5
            news = {}
            for q in range(Q):
                cx, cy, cz = CX[q], CY[q], CZ[q]
                if q == 0:
                    value = done[z + 1, 0]
                else:
                    source = z - cz
                    side = 0 if cx == 1 else 1
                    index = X_DIRS[side].index(q) if cx else None
                    value = moved(done[source + 1, q], finished, index, source, cx)
                    value = turn(value, cy, 0)
                    blocked = masks[source + 1, COMBOS.index((cx, cy))] > 0.5
                    value = jnp.where(blocked, done[z + 1, opposite[q]], value)
                    if cy == -1:
                        entering = inflow[incoming.index(q), pl.ds(z, 1), :]
                        value = jnp.where(height == planes - 1, entering, value)
                value = jnp.where(solid, current(step, q, z), value)
                if step == STEPS - 1:
                    out_ref[strided(q, z), :] = value
                else:
                    state[z, q] = value
                    news[q] = value
            if step < STEPS - 1:
                jx = functools.reduce(
                    lambda l, r: l + r, [news[p] - news[m] for p, m in zip(X_DIRS[0], X_DIRS[1])]
                )
                acc = acc + jx * (1.0 - flags[z + 1])
        if step < STEPS - 1:
            following = step + 1
            send_flow(following, acc)
            each_peer(lambda j: flow_copy(following, j).start())

            def edges():
                for side in range(2):
                    z_copy(following, side).start()

            collide_all(following, edges)
            for side, k in x_order:
                x_copy(following, side, k).start()

    for step in range(STEPS):
        for side in range(2):
            z_copy(step, side).wait_send()
        for side, k in x_order:
            x_copy(step, side, k).wait_send()
        pltpu.make_async_copy(a_recv.at[step], a_recv.at[step], a_send_sem.at[step]).wait()


def local(populations, solid, top_inflow):
    directions, planes, rows, width = populations.shape
    count_x, count_z = lax.axis_size("gx"), lax.axis_size("gz")
    assert X_FIELDS * rows <= width and count_x > 2 and count_z > 2
    devices = count_x * count_z
    tile = (planes, width)
    f32 = jnp.float32
    result = pl.pallas_call(
        functools.partial(kernel, (planes, rows, width, count_x, count_z)),
        out_shape=jax.ShapeDtypeStruct((directions * planes * rows, width), f32),
        in_specs=[pl.BlockSpec(memory_space=pl.ANY)] * 3,
        out_specs=pl.BlockSpec(memory_space=pltpu.VMEM),
        scratch_shapes=[
            pltpu.VMEM((directions * planes * rows, width), f32),
            pltpu.VMEM((planes * rows, width), jnp.int32),
            pltpu.VMEM(top_inflow.shape, f32),
            pltpu.VMEM((rows + 2,) + tile, f32),
            pltpu.VMEM((rows + 2, len(COMBOS)) + tile, f32),
            pltpu.VMEM((rows, Q) + tile, f32),
            pltpu.VMEM((rows, 4) + tile, f32),
            pltpu.VMEM((rows + 2, Q) + tile, f32),
            pltpu.VMEM((rows, Q) + tile, f32),
            pltpu.VMEM((STEPS, 2, Z_FIELDS) + tile, f32),
            pltpu.VMEM((STEPS, 2, Z_FIELDS) + tile, f32),
            pltpu.VMEM((STEPS, 2) + tile, f32),
            pltpu.VMEM((STEPS, 2, 3) + tile, f32),
            pltpu.VMEM((STEPS, 1, width), f32),
            pltpu.VMEM((STEPS, devices - 1, 1, width), f32),
            pltpu.SemaphoreType.DMA((3,)),
            pltpu.SemaphoreType.DMA((STEPS, 2)),
            pltpu.SemaphoreType.DMA((STEPS, 2)),
            pltpu.SemaphoreType.DMA((STEPS, 2, 3)),
            pltpu.SemaphoreType.DMA((STEPS, 2, 3)),
            pltpu.SemaphoreType.DMA((STEPS,)),
            pltpu.SemaphoreType.DMA((STEPS,)),
        ],
        compiler_params=pltpu.CompilerParams(
            collective_id=0, has_side_effects=True, vmem_limit_bytes=32 * 1024 * 1024
        ),
    )(
        populations.reshape(directions * planes * rows, width),
        solid.reshape(planes * rows, width),
        top_inflow,
    )
    return result.reshape(populations.shape)


def solution(mesh):
    return jax.shard_map(
        local,
        mesh=mesh,
        in_specs=(P(None, None, "gz", "gx"), P(None, "gz", "gx"), P(None, "gz", "gx")),
        out_specs=P(None, None, "gz", "gx"),
        check_vma=False,
    )
```

time: 151 us -> 21 us (0.14)
  blocking collectives: 77.9 us -> 0 us
  starting transfers between devices: 20.7 us -> 0 us
  Pallas kernels: 0 us -> 17.4 us
  other arithmetic: 14.9 us -> 0 us
  local copies, waits for them, and re-layouts: 17.8 us -> 3.39 us
  waiting for transfers between devices: 14 us -> 0 us
  matrix products: 2.11 us -> 0 us
  between operations: 2.08 us -> 0.01 us
    psum x2 -> x0, blocking collectives: 77.9 us -> none  [total_flow(): return lax.psum(local_sum, ('gx', 'gz')) / node_total]
    ppermute x12 -> x0, starting transfers between devices: 20.7 us -> none  [the longest x6 18.6 us: extended(): lax.ppermute(lax.slice_in_dim(block, 0, width, axis=dim), axis, backward)]
    pallas_call x0 -> x1, Pallas kernels: none -> 17.4 us  [local(): pl.pallas_call(functools.partial(kernel, (planes, rows, width, count_x, c...]
    ppermute x12 -> x0, waiting for transfers between devices: 14 us -> none  [the longest x6 7.44 us: extended(): lax.ppermute(lax.slice_in_dim(block, block.shape[dim] - width, None, axis...]
    unnamed x78 -> x0, other arithmetic: 6.22 us -> none
    slice x9 -> x0, local copies, waits for them, and re-layouts: 5.63 us -> none  [the longest x5 2.5 us: extended(): lax.slice_in_dim(block, 0, width, axis=dim)]
    unnamed x55 -> x7, local copies, waits for them, and re-layouts: 8.54 us -> 3.39 us
    ppermute x4 -> x0, local copies, waits for them, and re-layouts: 3.59 us -> none  [the longest x2 2.18 us: extended(): lax.ppermute(lax.slice_in_dim(block, block.shape[dim] - width, None, axis...]
  transfers between devices with their start and end apart: 12 -> 0, of which waited for: 6 -> 0; matrix products, arithmetic and copies ran while one was open for 8% -> 0% of each run, Pallas kernels for 0% -> 0%
where the time goes in v1:
time: 21 us; the launch traced here: 20.8 us
  Pallas kernels  17.4 us (83%)
  local copies, waits for them, and re-layouts  3.39 us (16%)
    pallas_call x1, Pallas kernels, local(): pl.pallas_call(functools.partial(kernel, (planes, rows, width, count_x, c...  17.4 us
    unnamed x7, local copies, waits for them, and re-layouts  3.39 us

profile of v1, /device:TPU:0, one launch (start us, length us, event | category | flops | bytes accessed | tf_op | source)
XLA Modules:
  0.0 20.8 jit_solution(7657347098771402931)
XLA Ops:
  0.0 0.0 copy-start
  0.0 1.1 %copy-done = f32[19,8,8,128]{3,2,1,0:T(8,128)S(1)} copy-done((f32[19,8,8,128]{3,2,1,0:T(8,128)S(1)}, f32[19,8,8,128]{3,2,1,0:T(8,128)}, u32[]{:S(2)}) %copy-start) | copy-done | bytes 622616
  1.1 0.0 copy-start.1
  1.1 0.8 %copy-done.1 = s32[8,8,128]{2,1,0:T(8,128)S(1)} copy-done((s32[8,8,128]{2,1,0:T(8,128)S(1)}, s32[8,8,128]{2,1,0:T(8,128)}, u32[]{:S(2)}) %copy-start.1) | copy-done | bytes 32792
  1.8 0.0 copy-start.2
  1.8 0.7 %copy-done.2 = f32[5,8,128]{2,1,0:T(8,128)S(1)} copy-done((f32[5,8,128]{2,1,0:T(8,128)S(1)}, f32[5,8,128]{2,1,0:T(8,128)}, u32[]{:S(2)}) %copy-start.2) | copy-done | bytes 20504
  2.6 17.4 %shard_map.37 = f32[1216,128]{1,0:T(8,128)S(1)} custom-call(f32[1216,128]{1,0:T(8,128)S(1)} %bitcast.4, s32[64,128]{1,0:T(8,128)S(1)} %bitcast.5, f32[5,8,128]{2,1,0:T(8,128)S(1)} %copy-done.2), custom_call_target="tpu_custom_call" | custom-call | tf_op jit(solution)/shard_map/pallas_call | solution.py:423
  19.9 0.8 %copy.5 = f32[19,8,8,128]{3,2,1,0:T(8,128)} copy(f32[19,8,8,128]{3,2,1,0:T(8,128)S(1)} %bitcast.3) | data formatting | bytes 1245184
Async XLA Ops:
  0.0 1.1 %copy-start = (f32[19,8,8,128]{3,2,1,0:T(8,128)S(1)}, f32[19,8,8,128]{3,2,1,0:T(8,128)}, u32[]{:S(2)}) copy-start(f32[19,8,8,128]{3,2,1,0:T(8,128)} %param.3) | copy-start | bytes 1867780
  1.1 0.8 %copy-start.1 = (s32[8,8,128]{2,1,0:T(8,128)S(1)}, s32[8,8,128]{2,1,0:T(8,128)}, u32[]{:S(2)}) copy-start(s32[8,8,128]{2,1,0:T(8,128)} %param.4) | copy-start | bytes 98308
  1.8 0.7 %copy-start.2 = (f32[5,8,128]{2,1,0:T(8,128)S(1)}, f32[5,8,128]{2,1,0:T(8,128)}, u32[]{:S(2)}) copy-start(f32[5,8,128]{2,1,0:T(8,128)} %inflow_hbm.1) | copy-start | bytes 61444

commit v2 on v1

--- a/solution.py
+++ b/solution.py
@@ -422,8 +422,8 @@
     f32 = jnp.float32
     result = pl.pallas_call(
         functools.partial(kernel, (planes, rows, width, count_x, count_z)),
-        out_shape=jax.ShapeDtypeStruct((directions * planes * rows, width), f32),
-        in_specs=[pl.BlockSpec(memory_space=pl.ANY)] * 3,
+        out_shape=pltpu.VMEM((directions * planes * rows, width), f32),
+        in_specs=[pl.BlockSpec(memory_space=pltpu.HBM)] * 3,
         out_specs=pl.BlockSpec(memory_space=pltpu.VMEM),
         scratch_shapes=[
             pltpu.VMEM((directions * planes * rows, width), f32),
@@ -450,7 +450,7 @@
             pltpu.SemaphoreType.DMA((STEPS,)),
         ],
         compiler_params=pltpu.CompilerParams(
-            collective_id=0, has_side_effects=True, vmem_limit_bytes=32 * 1024 * 1024
+            collective_id=0, has_side_effects=True, vmem_limit_bytes=60_000_000
         ),
     )(
         populations.reshape(directions * planes * rows, width),

time: 21 us -> 18.1 us (0.86)
  local copies, waits for them, and re-layouts: 3.39 us -> 0.83 us
  Pallas kernels: 17.4 us -> 17.1 us
    unnamed x7 -> x1, local copies, waits for them, and re-layouts: 3.39 us -> 0.83 us
    pallas_call x1, Pallas kernels: 17.4 us -> 17.1 us  [local(): pl.pallas_call(functools.partial(kernel, (planes, rows, width, count_x, c...]
where the time goes in v2:
time: 18.1 us; the launch traced here: 18 us
  Pallas kernels  17.1 us (94%)
  local copies, waits for them, and re-layouts  0.83 us (5%)
    pallas_call x1, Pallas kernels, local(): pl.pallas_call(functools.partial(kernel, (planes, rows, width, count_x, c...  17.1 us
    unnamed x1, local copies, waits for them, and re-layouts  0.83 us

profile of v2, /device:TPU:0, one launch (start us, length us, event | category | flops | bytes accessed | tf_op | source)
XLA Modules:
  0.0 18.0 jit_solution(1723622708284148383)
XLA Ops:
  0.0 17.1 %shard_map.37 = f32[1216,128]{1,0:T(8,128)S(1)} custom-call(f32[1216,128]{1,0:T(8,128)} %bitcast.4, s32[64,128]{1,0:T(8,128)} %bitcast.5, f32[5,8,128]{2,1,0:T(8,128)} %inflow_hbm.1), custom_call_target="tpu_custom_call" | custom-call | tf_op jit(solution)/shard_map/pallas_call | solution.py:423
  17.1 0.8 %copy.5 = f32[19,8,8,128]{3,2,1,0:T(8,128)} copy(f32[19,8,8,128]{3,2,1,0:T(8,128)S(1)} %bitcast.3) | data formatting | bytes 1245184
